TPU v7x, 32 devices: a whole 2x2x4 slice. The times are simulated.
32 devices in a mesh: ctx: 8 (over z, y), head: 4 (over x, core).
Axes of the slice: x: 2, y: 2, z: 4, core: 2. Of those that a mesh axis runs over, the one named last changes fastest.
Arguments:
- queries: bfloat16 [8192, 16, 128], P('ctx', 'head'), may hold values from -240 to 240, as said below
- lookup_arrays: bfloat16 [8192, 4, 128], P('ctx', 'head'), may hold values from -6 to 6
- content_arrays: bfloat16 [8192, 4, 128], P('ctx', 'head'), may hold values from -6 to 6
- selection: int32 [16, 4, 6], P('ctx', 'head'), may hold values from 0 to 15, as said below
- final_mapping: bfloat16 [2048, 4096], P('head'), may hold values from -0.125 to 0.125
Outputs:
- layer_out: bfloat16 [8192, 4096], P(('ctx', 'head'))
Inputs may be any that keep to these rules, and one draw needn't show every extreme that they name: `queries`: entries lie within -240 and 240. selection[b, h, :] holds 6 block numbers no larger than b; those smaller than b are distinct, and an entry equal to b names nothing. For each KV head and each index c of ctx, the selections of the 2 blocks held at c name, among the blocks held at any one index below c, at most one distinct block, and this bound is met.
All inputs are finite; a program needn't handle non-finite values.
Results may differ from a plain program's by a relative error of at most 0.01.
Values may be sent and summed in bfloat16 or wider, within the bound.
A program may use at most 128 MiB of HBM per device.

v0:
```python
import functools

import jax
import jax.numpy as jnp
from jax import lax
from jax.experimental import pallas as pl
from jax.experimental.pallas import tpu as pltpu
from jax.sharding import PartitionSpec as P

LOG2E = 1.4426950408889634


def fold(query, keys, values, carry, alive=None, allowed=None):
    factor = query.shape[1] ** (-0.5) * LOG2E
    scores = lax.dot_general(
        query, keys, (((1,), (1,)), ((), ())), preferred_element_type=jnp.float32
    )
    if carry is None:
        scores = jnp.where(allowed, scores, -jnp.inf)
        higher = pivot = jnp.max(scores, axis=1, keepdims=True)
    else:
        here = jnp.where(alive, jnp.max(scores, axis=1, keepdims=True), -jnp.inf)
        higher = jnp.maximum(carry[0], here)
        pivot = jnp.where(alive, higher, jnp.float32(1e30))
    weights = jnp.exp2((scores - pivot) * factor)
    total = jnp.sum(weights, axis=1, keepdims=True)
    mixed = jnp.dot(weights.astype(jnp.bfloat16), values, preferred_element_type=jnp.float32)
    if carry is None:
        return higher, total, mixed
    keep = jnp.exp2((carry[0] - higher) * factor)
    return higher, carry[1] * keep + total, carry[2] * keep + mixed


def stage_kernel(own, resumed, last, count, slots, live, q_ref, *refs):
    block = pl.program_id(0)
    sources = refs[:count]
    refs = refs[count:]
    query = q_ref[...]
    rows = query.shape[0]
    if resumed:
        carry = (refs[1][:, 0:1], refs[1][:, 1:2], refs[0][...])
        refs = refs[2:]
    else:
        row = lax.broadcasted_iota(jnp.int32, (rows, rows), 0)
        column = lax.broadcasted_iota(jnp.int32, (rows, rows), 1)
        carry = fold(query, sources[0][0, block], sources[0][1, block], None, None, row >= column)
    for slot in range(slots.shape[1]):
        source = sources[0 if own else slot]
        place = slots[block, slot]
        alive = live[block, slot] > 0
        carry = fold(query, source[0, place], source[1, place], carry, alive)
    peak, total, mixed = carry
    if last:
        refs[0][...] = (mixed / total).astype(jnp.bfloat16)
    else:
        refs[0][...] = mixed
        lane = lax.broadcasted_iota(jnp.int32, mixed.shape, 1)
        refs[1][...] = jnp.where(lane == 0, peak, total)


def attend_stage(queries, sources, slots, live, state, last):
    blocks = slots.shape[0]
    rows = queries.shape[0] // blocks
    depth = sources[0].shape[-1]
    heads = queries.shape[1] // depth
    tile = pl.BlockSpec((rows, depth), lambda b, h, *_: (b, h))
    wholes = [pl.BlockSpec(s.shape, lambda b, h, *_: (0, 0, 0, 0)) for s in sources]
    shape = jax.ShapeDtypeStruct(queries.shape, jnp.float32)
    return pl.pallas_call(
        functools.partial(stage_kernel, state is None, state is not None, last, len(sources)),
        out_shape=jax.ShapeDtypeStruct(queries.shape, jnp.bfloat16) if last else (shape, shape),
        grid_spec=pltpu.PrefetchScalarGridSpec(
            num_scalar_prefetch=2,
            grid=(blocks, heads),
            in_specs=[tile] + wholes + [tile] * (0 if state is None else 2),
            out_specs=tile if last else (tile, tile),
        ),
        compiler_params=pltpu.CompilerParams(vmem_limit_bytes=24 * 1024 * 1024),
        cost_estimate=pl.CostEstimate(
            flops=8 * rows * rows * depth * heads * slots.size,
            bytes_accessed=4 * queries.size,
            transcendentals=rows * rows * heads * slots.size,
        ),
    )(slots, live, queries, *sources, *(state or ()))


CUTS = 2


def swap(array, axis, offset):
    size = lax.axis_size(axis)
    return lax.ppermute(array, axis, [(i, i ^ offset) for i in range(size)])


def gather_mapping(mapping):
    count = lax.axis_size("head")
    half = mapping.shape[0] // 2
    depth = half // CUTS
    side = lax.axis_index("ctx") % 2
    held = {0: [(mapping, None, 0)]}
    far = []
    for cut in range(CUTS):
        mine = lax.dynamic_slice_in_dim(mapping, side * half + cut * depth, depth, 0)
        near = swap(mine, "head", count // 2)
        far.append((near, 0, cut * depth))
        far.append((swap(near, "ctx", 1), 1, cut * depth))
    held[count // 2] = far
    step = count // 4
    while step:
        for offset, pieces in list(held.items()):
            held[offset ^ step] = []
            for piece, side_of, row in pieces:
                held[offset ^ step].append((swap(piece, "head", step), side_of, row))
        step //= 2
    return held


def project_kernel(plan, half, side_ref, *refs):
    count = len(plan)
    rows = refs[:count]
    pieces = refs[count:-1]
    out_ref = refs[-1]
    side = side_ref[0]
    total = None
    at = 0
    for offset, entries in enumerate(plan):
        for where, start in entries:
            piece = pieces[at]
            at += 1
            depth = piece.shape[0]
            if where is None:
                left = rows[offset][...]
            else:
                own = side if where == 0 else 1 - side
                column = pl.multiple_of(own * half + start, 128)
                left = rows[offset][:, pl.ds(column, depth)]
            term = jnp.dot(left, piece[...], preferred_element_type=jnp.float32)
            total = term if total is None else total + term
    out_ref[...] = total.astype(jnp.bfloat16)


def project(rows, held):
    count = len(rows)
    plan = tuple(tuple((s, r) for _, s, r in held[offset]) for offset in range(count))
    pieces = [p for offset in range(count) for p, _, _ in held[offset]]
    tokens, depth = rows[0].shape
    width = pieces[0].shape[1]
    tile = min(512, width)
    side = (lax.axis_index("ctx") % 2).astype(jnp.int32).reshape(1)
    return pl.pallas_call(
        functools.partial(project_kernel, plan, depth // 2),
        out_shape=jax.ShapeDtypeStruct((tokens, width), jnp.bfloat16),
        grid_spec=pltpu.PrefetchScalarGridSpec(
            num_scalar_prefetch=1,
            grid=(width // tile,),
            in_specs=[pl.BlockSpec((tokens, depth), lambda j, *_: (0, 0))] * count
            + [pl.BlockSpec((p.shape[0], tile), lambda j, *_: (0, j)) for p in pieces],
            out_specs=pl.BlockSpec((tokens, tile), lambda j, *_: (0, j)),
        ),
        compiler_params=pltpu.CompilerParams(vmem_limit_bytes=24 * 1024 * 1024),
        cost_estimate=pl.CostEstimate(
            flops=2 * tokens * depth * count * width,
            bytes_accessed=2 * depth * count * width,
            transcendentals=0,
        ),
        name="project",
    )(side, *rows, *pieces)


def whole_body(queries, lookup_arrays, content_arrays, selection, final_mapping):
    ctx_count = lax.axis_size("ctx")
    position = lax.axis_index("ctx")
    blocks_here = selection.shape[0]
    tokens_here = queries.shape[0]
    block_size = tokens_here // blocks_here
    head_dim = queries.shape[2]
    stacked = jnp.stack(
        [
            lookup_arrays.reshape(blocks_here, block_size, head_dim),
            content_arrays.reshape(blocks_here, block_size, head_dim),
        ]
    )
    chosen = selection[:, 0, :]
    holders = chosen // blocks_here
    first_here = position * blocks_here

    def wanted_from(owner):
        match = (holders == owner) & (owner >= 0) & (owner < position)
        places = jnp.max(jnp.where(match, chosen - owner * blocks_here, -1), axis=1)
        return jnp.maximum(places, 0), (places >= 0).astype(jnp.int32)

    peers = jnp.arange(ctx_count, dtype=jnp.int32)
    matches = (holders[:, :, None] == peers) & (peers < position)
    wanted = jnp.max(
        jnp.where(matches, chosen[:, :, None] - peers * blocks_here, 0), axis=(0, 1)
    )
    asked = swap(wanted.astype(jnp.int32), "ctx", 1)
    forward = [(i, i + 2) for i in range(ctx_count - 2)]
    rounds = ctx_count // 2 - 1
    chain = [stacked]
    sides = []
    for turn in range(rounds + 1):
        if turn:
            chain.append(lax.ppermute(chain[-1], "ctx", forward))
        owner = jnp.maximum(position - 2 * turn, 0)
        place = lax.dynamic_index_in_dim(asked, owner, 0, keepdims=False)
        picked = lax.dynamic_slice_in_dim(chain[-1], place, 1, 1)
        sides.append(swap(picked, "ctx", 1))
    held = gather_mapping(final_mapping)

    flat_queries = queries.reshape(tokens_here, -1)
    inside = jnp.arange(blocks_here, dtype=jnp.int32)
    slots = jnp.broadcast_to(inside[None, :], (blocks_here, blocks_here))
    named = jnp.any(chosen[:, :, None] == first_here + inside, axis=1)
    live = named & (inside[None, :] < inside[:, None])
    state = attend_stage(flat_queries, [stacked], slots, live.astype(jnp.int32), None, False)
    twin = position ^ 1
    for turn in range(1, rounds + 2):
        direct, direct_live = wanted_from(position - 2 * turn)
        _, side_live = wanted_from(twin - 2 * (turn - 1))
        none = jnp.zeros_like(direct)
        last = turn == rounds + 1
        sources = [sides[turn - 1]] if last else [chain[turn], sides[turn - 1]]
        places = [none] if last else [direct, none]
        lives = [side_live] if last else [direct_live, side_live]
        state = attend_stage(
            flat_queries, sources, jnp.stack(places, axis=1), jnp.stack(lives, axis=1), state, last
        )
    flat_rows = state
    head_count = lax.axis_size("head")
    head = lax.axis_index("head")
    tokens_out = tokens_here // head_count
    rows = []
    for offset in range(head_count):
        part = lax.dynamic_slice_in_dim(flat_rows, (head ^ offset) * tokens_out, tokens_out, 0)
        rows.append(swap(part, "head", offset) if offset else part)
    return project(rows, held)


def solution(mesh):
    in_specs = (
        P("ctx", "head", None),
        P("ctx", "head", None),
        P("ctx", "head", None),
        P("ctx", "head", None),
        P("head", None),
    )
    out_specs = P(("ctx", "head"), None)
    return jax.shard_map(whole_body, mesh=mesh, in_specs=in_specs, out_specs=out_specs, check_vma=False)
```

profile of v0, /device:TPU:0, one launch (start us, length us, event | category | flops | bytes accessed | tf_op | source)
XLA Modules:
  0.0 192.6 jit_solution(430510156346701308)
XLA Ops:
  1.8 3.1 %collective-permute-start.3 = (s32[8]{0:T(128)S(1)}, s32[8]{0:T(128)S(1)}, u32[]{:S(2)}, u32[]{:S(2)}) collective-permute-start(s32[8]{0:T(128)S(1)} %fusion.1), channel_id=1, source_target_pairs={{0,4},{4,0},{8,12},{12,8},{16,20},{20,16},{24,28},{28,24},{1,5},{5... | collective-permute-start | bytes 104 | tf_op jit(solution)/shard_map/ppermute | solution.py:92
  4.9 1.9 pad_maximum_fusion.refs_0_
  6.8 4.3 %collective-permute-start = (bf16[2,2,512,128]{3,2,1,0:T(8,128)(2,1)}, bf16[2,2,512,128]{3,2,1,0:T(8,128)(2,1)}, u32[]{:S(2)}, u32[]{:S(2)}) collective-permute-start(bf16[2,2,512,128]{3,2,1,0:T(8,128)(2,1)} %pad_maximum_fusion.refs_0_), channel_id=1, source_target_pairs={{0,8},{4,12},{8,16},{12,20},{16,24},{20,28},{1,9},{5,13},{9,17},{1... | collective-permute-start | bytes 1572872 | tf_op jit(solution)/shard_map/ppermute | solution.py:204
  11.1 3.1 %constant_dynamic-slice_fusion = (bf16[128,4096]{1,0:T(8,128)(2,1)}, bf16[128,4096]{1,0:T(8,128)(2,1)}) fusion(bf16[512,4096]{1,0:T(8,128)(2,1)} %refs_4_.1, s32[]{:T(128)S(6)} %select_n.98, s32[]{:T(128)S(6)} %select_n.97), kind=kLoop, calls=%fused_computation.8 | loop fusion | bytes 4194312 | tf_op jit(solution)/shard_map/dynamic_slice | solution.py:103
  14.2 1.5 collective-permute-start.12
  16.4 1.4 copy.30
  18.1 12.8 %shard_map.55 = (f32[1024,512]{1,0:T(8,128)S(1)}, f32[1024,512]{1,0:T(8,128)S(1)}) custom-call(s32[2,2]{1,0:T(2,128)S(1)} %broadcast_in_dim.28.slots, s32[2,2]{1,0:T(2,128)S(1)} %and_convert_fusion.live, bf16[1024,512]{1,0:T(8,128)(2,1)S(1)} %bitcast.32, bf16[2,2,512,128]{3,2,1,0:T(8,128)(2,1)} %pad_maximum_fusion.refs_0_), custom_call_target="tpu_custom_call" | custom-call | flops 4294967296 | bytes 2097152 | tf_op jit(solution)/shard_map/pallas_call | solution.py:69
  32.2 1.3 copy-done.3
  34.0 3.6 %collective-permute-start.1 = (bf16[2,2,512,128]{3,2,1,0:T(8,128)(2,1)}, bf16[2,2,512,128]{3,2,1,0:T(8,128)(2,1)}, u32[]{:S(2)}, u32[]{:S(2)}) collective-permute-start(bf16[2,2,512,128]{3,2,1,0:T(8,128)(2,1)} %collective-permute-done.refs_0_), channel_id=1, source_target_pairs={{0,8},{4,12},{8,16},{12,20},{16,24},{20,28},{1,9},{5,13},{9,17},{1... | collective-permute-start | bytes 1572872 | tf_op jit(solution)/shard_map/ppermute | solution.py:204
  40.2 1.6 fusion
  51.0 2.9 %collective-permute-start.2 = (bf16[2,2,512,128]{3,2,1,0:T(8,128)(2,1)}, bf16[2,2,512,128]{3,2,1,0:T(8,128)(2,1)S(1)}, u32[]{:S(2)}, u32[]{:S(2)}) collective-permute-start(bf16[2,2,512,128]{3,2,1,0:T(8,128)(2,1)} %collective-permute-done.1.refs_0_), channel_id=1, source_target_pairs={{0,8},{4,12},{8,16},{12,20},{16,24},{20,28},{1,9},{5,13},{9,17},{1... | collective-permute-start | bytes 1572872 | tf_op jit(solution)/shard_map/ppermute | solution.py:204
  53.9 1.6 copy-done.2
  55.4 1.6 copy-done.4
  57.0 27.5 %shard_map.56 = (f32[1024,512]{1,0:T(8,128)S(1)}, f32[1024,512]{1,0:T(8,128)S(1)}) custom-call(s32[2,2]{1,0:T(2,128)S(1)} %stack.44.slots, s32[2,2]{1,0:T(2,128)S(1)} %add_convert_fusion.2.live, bf16[1024,512]{1,0:T(8,128)(2,1)S(1)} %bitcast.33, bf16[2,2,512,128]{3,2,1,0:T(8,128)(2,1)} %collective-permute-done.refs_0_, ...), custom_call_target="tpu_custom_call" | custom-call | flops 4294967296 | bytes 2097152 | tf_op jit(solution)/shard_map/pallas_call | solution.py:69
  88.6 27.5 %shard_map.57 = (f32[1024,512]{1,0:T(8,128)S(1)}, f32[1024,512]{1,0:T(8,128)S(1)}) custom-call(s32[2,2]{1,0:T(2,128)S(1)} %stack.41.slots, s32[2,2]{1,0:T(2,128)S(1)} %add_convert_fusion.1.live, bf16[1024,512]{1,0:T(8,128)(2,1)S(1)} %bitcast.34, bf16[2,2,512,128]{3,2,1,0:T(8,128)(2,1)} %collective-permute-done.1.refs_0_, ...), custom_call_target="tpu_custom_call" | custom-call | flops 4294967296 | bytes 2097152 | tf_op jit(solution)/shard_map/pallas_call | solution.py:69
  117.2 26.5 %shard_map.58 = (f32[1024,512]{1,0:T(8,128)S(1)}, f32[1024,512]{1,0:T(8,128)S(1)}) custom-call(s32[2,2]{1,0:T(2,128)S(1)} %stack.38.slots, s32[2,2]{1,0:T(2,128)S(1)} %add_convert_fusion.live, bf16[1024,512]{1,0:T(8,128)(2,1)S(1)} %bitcast.35, bf16[2,2,512,128]{3,2,1,0:T(8,128)(2,1)S(1)} %collective-permute-done.2.refs_0_, ...), custom_call_target="tpu_custom_call" | custom-call | flops 4294967296 | bytes 2097152 | tf_op jit(solution)/shard_map/pallas_call | solution.py:69
  143.8 15.6 %shard_map.59 = bf16[1024,512]{1,0:T(8,128)(2,1)S(1)} custom-call(s32[2,1]{1,0:T(2,128)S(1)} %broadcast_7_slots.2.slots, s32[2,1]{1,0:T(2,128)S(1)} %copy.27.live, bf16[1024,512]{1,0:T(8,128)(2,1)S(1)} %bitcast.36, bf16[2,1,512,128]{3,2,1,0:T(8,128)(2,1)S(1)} %collective-permute-done.4.refs_0_, f32[1024,512]{1,0:T(8,128)S(1)} %get-tuple-element.19.refs_1_, ...), custom_call_target="tpu_custom_call" | custom-call | flops 2147483648 | bytes 2097152 | tf_op jit(solution)/shard_map/pallas_call | solution.py:69
  159.6 1.6 collective-permute-start.8
  161.2 7.0 %collective-permute-done.10.refs_3_ = bf16[256,512]{1,0:T(8,128)(2,1)S(1)} collective-permute-done((bf16[256,512]{1,0:T(8,128)(2,1)S(1)}, bf16[256,512]{1,0:T(8,128)(2,1)S(1)}, u32[]{:S(2)}, u32[]{:S(2)}) %collective-permute-start.10) | collective-permute-done | bytes 262176 | tf_op jit(solution)/shard_map/ppermute | solution.py:92
  168.8 7.7 %collective-permute-done.9.refs_2_ = bf16[256,512]{1,0:T(8,128)(2,1)S(1)} collective-permute-done((bf16[256,512]{1,0:T(8,128)(2,1)S(1)}, bf16[256,512]{1,0:T(8,128)(2,1)S(1)}, u32[]{:S(2)}, u32[]{:S(2)}) %collective-permute-start.9) | collective-permute-done | bytes 262176 | tf_op jit(solution)/shard_map/ppermute | solution.py:92
  177.1 2.1 %collective-permute-done.18.refs_12_ = bf16[128,4096]{1,0:T(8,128)(2,1)S(1)} collective-permute-done((bf16[128,4096]{1,0:T(8,128)(2,1)S(1)}, bf16[128,4096]{1,0:T(8,128)(2,1)S(1)}, u32[]{:S(2)}, u32[]{:S(2)}) %collective-permute-start.18) | collective-permute-done | bytes 1048608 | tf_op jit(solution)/shard_map/ppermute | solution.py:92
  179.1 1.5 collective-permute-done.17.refs_11_
  180.6 1.5 collective-permute-done.19.refs_13_
  182.1 10.5 %project.1 = bf16[256,4096]{1,0:T(8,128)(2,1)} custom-call(s32[1]{0:T(128)} %bitcast.side_ref, bf16[256,512]{1,0:T(8,128)(2,1)S(1)} %get-tuple-element.34.refs_0_, bf16[256,512]{1,0:T(8,128)(2,1)S(1)} %collective-permute-done.8.refs_1_, bf16[256,512]{1,0:T(8,128)(2,1)S(1)} %collective-permute-done.9.refs_2_, ...), custom_call_target="tpu_custom_call" | custom-call | flops 4294967296 | bytes 16777216 | tf_op jit(solution)/shard_map/project/pallas_call | solution.py:150
  (79 shorter events, 15.6 us)
Async XLA Ops:
  1.8 35.9 %collective-permute-start.3 = (s32[8]{0:T(128)S(1)}, s32[8]{0:T(128)S(1)}, u32[]{:S(2)}, u32[]{:S(2)}) collective-permute-start(s32[8]{0:T(128)S(1)} %fusion.1), channel_id=1, source_target_pairs={{0,4},{4,0},{8,12},{12,8},{16,20},{20,16},{24,28},{28,24},{1,5},{5... | collective-permute-start | bytes 104 | tf_op jit(solution)/shard_map/ppermute | solution.py:92
  6.8 27.2 %collective-permute-start = (bf16[2,2,512,128]{3,2,1,0:T(8,128)(2,1)}, bf16[2,2,512,128]{3,2,1,0:T(8,128)(2,1)}, u32[]{:S(2)}, u32[]{:S(2)}) collective-permute-start(bf16[2,2,512,128]{3,2,1,0:T(8,128)(2,1)} %pad_maximum_fusion.refs_0_), channel_id=1, source_target_pairs={{0,8},{4,12},{8,16},{12,20},{16,24},{20,28},{1,9},{5,13},{9,17},{1... | collective-permute-start | bytes 1572872 | tf_op jit(solution)/shard_map/ppermute | solution.py:204
  11.1 171.0 %collective-permute-start.11 = (bf16[512,4096]{1,0:T(8,128)(2,1)}, bf16[512,4096]{1,0:T(8,128)(2,1)}, u32[]{:S(2)}, u32[]{:S(2)}) collective-permute-start(bf16[512,4096]{1,0:T(8,128)(2,1)} %refs_4_.1), channel_id=1, source_target_pairs={{0,1},{1,0},{2,3},{3,2},{4,5},{5,4},{6,7},{7,6},{8,9},{9,8},{10,11... | collective-permute-start | bytes 12582920 | tf_op jit(solution)/shard_map/ppermute | solution.py:92
  11.1 5.2 %copy-start.6 = (s32[2,1,6]{2,1,0:T(1,128)S(1)}, s32[2,1,6]{2,1,0:T(1,128)}, u32[]{:S(2)}) copy-start(s32[2,1,6]{2,1,0:T(1,128)} %param.8) | copy-start | bytes 148
  14.2 72.3 %collective-permute-start.12 = (bf16[128,4096]{1,0:T(8,128)(2,1)}, bf16[128,4096]{1,0:T(8,128)(2,1)S(1)}, u32[]{:S(2)}, u32[]{:S(2)}) collective-permute-start(bf16[128,4096]{1,0:T(8,128)(2,1)} %get-tuple-element.30), channel_id=1, source_target_pairs={{0,2},{1,3},{2,0},{3,1},{4,6},{5,7},{6,4},{7,5},{8,10},{9,11},{10,... | collective-permute-start | bytes 3145736 | tf_op jit(solution)/shard_map/ppermute | solution.py:92
  15.7 71.9 %collective-permute-start.14 = (bf16[128,4096]{1,0:T(8,128)(2,1)}, bf16[128,4096]{1,0:T(8,128)(2,1)S(1)}, u32[]{:S(2)}, u32[]{:S(2)}) collective-permute-start(bf16[128,4096]{1,0:T(8,128)(2,1)} %get-tuple-element.29), channel_id=1, source_target_pairs={{0,2},{1,3},{2,0},{3,1},{4,6},{5,7},{6,4},{7,5},{8,10},{9,11},{10,... | collective-permute-start | bytes 3145736 | tf_op jit(solution)/shard_map/ppermute | solution.py:92
  18.1 22.2 %copy-start.5 = (bf16[1024,1,128]{2,0,1:T(8,128)(2,1)S(1)}, bf16[1024,1,128]{2,0,1:T(8,128)(2,1)}, u32[]{:S(2)}) copy-start(bf16[1024,1,128]{2,0,1:T(8,128)(2,1)} %param.7) | copy-start | bytes 786436
  34.0 17.0 %collective-permute-start.1 = (bf16[2,2,512,128]{3,2,1,0:T(8,128)(2,1)}, bf16[2,2,512,128]{3,2,1,0:T(8,128)(2,1)}, u32[]{:S(2)}, u32[]{:S(2)}) collective-permute-start(bf16[2,2,512,128]{3,2,1,0:T(8,128)(2,1)} %collective-permute-done.refs_0_), channel_id=1, source_target_pairs={{0,8},{4,12},{8,16},{12,20},{16,24},{20,28},{1,9},{5,13},{9,17},{1... | collective-permute-start | bytes 1572872 | tf_op jit(solution)/shard_map/ppermute | solution.py:204
  41.9 8.0 %collective-permute-start.7 = (bf16[2,1,512,128]{3,2,1,0:T(8,128)(2,1)}, bf16[2,1,512,128]{3,2,1,0:T(8,128)(2,1)S(1)}, u32[]{:S(2)}, u32[]{:S(2)}) collective-permute-start(bf16[2,1,512,128]{3,2,1,0:T(8,128)(2,1)} %fusion), channel_id=1, source_target_pairs={{0,4},{4,0},{8,12},{12,8},{16,20},{20,16},{24,28},{28,24},{1,5},{5... | collective-permute-start | bytes 786440 | tf_op jit(solution)/shard_map/ppermute | solution.py:92
  49.9 35.6 %collective-permute-start.6 = (bf16[2,1,512,128]{3,2,1,0:T(8,128)(2,1)S(1)}, bf16[2,1,512,128]{3,2,1,0:T(8,128)(2,1)S(1)}, u32[]{:S(2)}, u32[]{:S(2)}) collective-permute-start(bf16[2,1,512,128]{3,2,1,0:T(8,128)(2,1)S(1)} %constant_dynamic-slice_fusion.6), channel_id=1, source_target_pairs={{0,4},{4,0},{8,12},{12,8},{16,20},{20,16},{24,28},{28,24},{1,5},{5... | collective-permute-start | bytes 786440 | tf_op jit(solution)/shard_map/ppermute | solution.py:92
  51.0 65.1 %collective-permute-start.2 = (bf16[2,2,512,128]{3,2,1,0:T(8,128)(2,1)}, bf16[2,2,512,128]{3,2,1,0:T(8,128)(2,1)S(1)}, u32[]{:S(2)}, u32[]{:S(2)}) collective-permute-start(bf16[2,2,512,128]{3,2,1,0:T(8,128)(2,1)} %collective-permute-done.1.refs_0_), channel_id=1, source_target_pairs={{0,8},{4,12},{8,16},{12,20},{16,24},{20,28},{1,9},{5,13},{9,17},{1... | collective-permute-start | bytes 1572872 | tf_op jit(solution)/shard_map/ppermute | solution.py:204
  53.8 1.6 copy-start.2
  85.5 31.7 %collective-permute-start.5 = (bf16[2,1,512,128]{3,2,1,0:T(8,128)(2,1)S(1)}, bf16[2,1,512,128]{3,2,1,0:T(8,128)(2,1)S(1)}, u32[]{:S(2)}, u32[]{:S(2)}) collective-permute-start(bf16[2,1,512,128]{3,2,1,0:T(8,128)(2,1)S(1)} %constant_dynamic-slice_fusion.7), channel_id=1, source_target_pairs={{0,4},{4,0},{8,12},{12,8},{16,20},{20,16},{24,28},{28,24},{1,5},{5... | collective-permute-start | bytes 786440 | tf_op jit(solution)/shard_map/ppermute | solution.py:92
  86.6 89.9 %collective-permute-start.13 = (bf16[128,4096]{1,0:T(8,128)(2,1)S(1)}, bf16[128,4096]{1,0:T(8,128)(2,1)S(1)}, u32[]{:S(2)}, u32[]{:S(2)}) collective-permute-start(bf16[128,4096]{1,0:T(8,128)(2,1)S(1)} %collective-permute-done.12.refs_6_), channel_id=1, source_target_pairs={{0,4},{4,0},{8,12},{12,8},{16,20},{20,16},{24,28},{28,24},{1,5},{5... | collective-permute-start | bytes 3145736 | tf_op jit(solution)/shard_map/ppermute | solution.py:92
  87.6 89.4 %collective-permute-start.15 = (bf16[128,4096]{1,0:T(8,128)(2,1)S(1)}, bf16[128,4096]{1,0:T(8,128)(2,1)S(1)}, u32[]{:S(2)}, u32[]{:S(2)}) collective-permute-start(bf16[128,4096]{1,0:T(8,128)(2,1)S(1)} %collective-permute-done.14.refs_8_), channel_id=1, source_target_pairs={{0,4},{4,0},{8,12},{12,8},{16,20},{20,16},{24,28},{28,24},{1,5},{5... | collective-permute-start | bytes 3145736 | tf_op jit(solution)/shard_map/ppermute | solution.py:92
  116.1 27.6 %collective-permute-start.4 = (bf16[2,1,512,128]{3,2,1,0:T(8,128)(2,1)S(1)}, bf16[2,1,512,128]{3,2,1,0:T(8,128)(2,1)S(1)}, u32[]{:S(2)}, u32[]{:S(2)}) collective-permute-start(bf16[2,1,512,128]{3,2,1,0:T(8,128)(2,1)S(1)} %constant_dynamic-slice_fusion.8), channel_id=1, source_target_pairs={{0,4},{4,0},{8,12},{12,8},{16,20},{20,16},{24,28},{28,24},{1,5},{5... | collective-permute-start | bytes 786440 | tf_op jit(solution)/shard_map/ppermute | solution.py:92
  143.8 38.3 %copy-start = (bf16[512,4096]{1,0:T(8,128)(2,1)S(1)}, bf16[512,4096]{1,0:T(8,128)(2,1)}, u32[]{:S(2)}) copy-start(bf16[512,4096]{1,0:T(8,128)(2,1)} %refs_4_.1) | copy-start | bytes 12582916
  159.5 8.6 %collective-permute-start.10 = (bf16[256,512]{1,0:T(8,128)(2,1)S(1)}, bf16[256,512]{1,0:T(8,128)(2,1)S(1)}, u32[]{:S(2)}, u32[]{:S(2)}) collective-permute-start(bf16[256,512]{1,0:T(8,128)(2,1)S(1)} %get-tuple-element.31), channel_id=1, source_target_pairs={{0,3},{1,2},{2,1},{3,0},{4,7},{5,6},{6,5},{7,4},{8,11},{9,10},{10,... | collective-permute-start | bytes 786440 | tf_op jit(solution)/shard_map/ppermute | solution.py:92
  159.6 9.2 %collective-permute-start.8 = (bf16[256,512]{1,0:T(8,128)(2,1)S(1)}, bf16[256,512]{1,0:T(8,128)(2,1)S(1)}, u32[]{:S(2)}, u32[]{:S(2)}) collective-permute-start(bf16[256,512]{1,0:T(8,128)(2,1)S(1)} %get-tuple-element.33), channel_id=1, source_target_pairs={{0,1},{1,0},{2,3},{3,2},{4,5},{5,4},{6,7},{7,6},{8,9},{9,8},{10,11... | collective-permute-start | bytes 786440 | tf_op jit(solution)/shard_map/ppermute | solution.py:92
  168.1 8.3 %collective-permute-start.9 = (bf16[256,512]{1,0:T(8,128)(2,1)S(1)}, bf16[256,512]{1,0:T(8,128)(2,1)S(1)}, u32[]{:S(2)}, u32[]{:S(2)}) collective-permute-start(bf16[256,512]{1,0:T(8,128)(2,1)S(1)} %get-tuple-element.32), channel_id=1, source_target_pairs={{0,2},{1,3},{2,0},{3,1},{4,6},{5,7},{6,4},{7,5},{8,10},{9,11},{10,... | collective-permute-start | bytes 786440 | tf_op jit(solution)/shard_map/ppermute | solution.py:92
  168.8 8.3 %collective-permute-start.16 = (bf16[128,4096]{1,0:T(8,128)(2,1)S(1)}, bf16[128,4096]{1,0:T(8,128)(2,1)S(1)}, u32[]{:S(2)}, u32[]{:S(2)}) collective-permute-start(bf16[128,4096]{1,0:T(8,128)(2,1)S(1)} %collective-permute-done.12.refs_6_), channel_id=1, source_target_pairs={{0,1},{1,0},{2,3},{3,2},{4,5},{5,4},{6,7},{7,6},{8,9},{9,8},{10,11... | collective-permute-start | bytes 3145736 | tf_op jit(solution)/shard_map/ppermute | solution.py:92
  176.5 2.7 %collective-permute-start.18 = (bf16[128,4096]{1,0:T(8,128)(2,1)S(1)}, bf16[128,4096]{1,0:T(8,128)(2,1)S(1)}, u32[]{:S(2)}, u32[]{:S(2)}) collective-permute-start(bf16[128,4096]{1,0:T(8,128)(2,1)S(1)} %collective-permute-done.14.refs_8_), channel_id=1, source_target_pairs={{0,1},{1,0},{2,3},{3,2},{4,5},{5,4},{6,7},{7,6},{8,9},{9,8},{10,11... | collective-permute-start | bytes 3145736 | tf_op jit(solution)/shard_map/ppermute | solution.py:92
  176.5 4.2 %collective-permute-start.17 = (bf16[128,4096]{1,0:T(8,128)(2,1)S(1)}, bf16[128,4096]{1,0:T(8,128)(2,1)S(1)}, u32[]{:S(2)}, u32[]{:S(2)}) collective-permute-start(bf16[128,4096]{1,0:T(8,128)(2,1)S(1)} %collective-permute-done.13.refs_7_), channel_id=1, source_target_pairs={{0,1},{1,0},{2,3},{3,2},{4,5},{5,4},{6,7},{7,6},{8,9},{9,8},{10,11... | collective-permute-start | bytes 3145736 | tf_op jit(solution)/shard_map/ppermute | solution.py:92
  177.0 5.1 %collective-permute-start.19 = (bf16[128,4096]{1,0:T(8,128)(2,1)S(1)}, bf16[128,4096]{1,0:T(8,128)(2,1)S(1)}, u32[]{:S(2)}, u32[]{:S(2)}) collective-permute-start(bf16[128,4096]{1,0:T(8,128)(2,1)S(1)} %collective-permute-done.15.refs_9_), channel_id=1, source_target_pairs={{0,1},{1,0},{2,3},{3,2},{4,5},{5,4},{6,7},{7,6},{8,9},{9,8},{10,11... | collective-permute-start | bytes 3145736 | tf_op jit(solution)/shard_map/ppermute | solution.py:92
  (3 other events, 4.2 us)
where the time goes:
time: 193 us
  Pallas kernels  120 us (62%)
  starting transfers between devices  24.4 us (13%)
  waiting for transfers between devices  20.3 us (11%)
  local copies, waits for them, and re-layouts  15 us (8%)
  between operations  7.37 us (4%)
  other arithmetic  5.1 us (3%)
    pallas_call x5, Pallas kernels, attend_stage(): pl.pallas_call(functools.partial(stage_kernel, state is None, state is no...  110 us
    ppermute x17, waiting for transfers between devices, swap(): return lax.ppermute(array, axis, [(i, i ^ offset) for i in range(size)])  20.3 us
    ppermute x17, starting transfers between devices, swap(): return lax.ppermute(array, axis, [(i, i ^ offset) for i in range(size)])  13.7 us
    ppermute x3, starting transfers between devices, whole_body(): chain.append(lax.ppermute(chain[-1], 'ctx', forward))  10.8 us
    pallas_call x1, Pallas kernels, project(): pl.pallas_call(functools.partial(project_kernel, plan, depth // 2), out_s...  10.5 us
    unnamed x15, local copies, waits for them, and re-layouts  7.24 us
  transfers between devices with their start and end apart: 20, of which 6 were waited for; matrix products, arithmetic and copies ran while one was open for 6% of the time, Pallas kernels for 57%

commit v1 on v0

--- a/solution.py
+++ b/solution.py
@@ -10,20 +10,27 @@
 LOG2E = 1.4426950408889634
 
 
+def widen(column, width):
+    return jnp.concatenate([column] * (width // column.shape[1]), axis=1)
+
+
 def fold(query, keys, values, carry, alive=None, allowed=None):
-    factor = query.shape[1] ** (-0.5) * LOG2E
+    shape = query.shape
+    factor = shape[1] ** (-0.5) * LOG2E
     scores = lax.dot_general(
         query, keys, (((1,), (1,)), ((), ())), preferred_element_type=jnp.float32
     )
+    width = scores.shape[1]
     if carry is None:
         scores = jnp.where(allowed, scores, -jnp.inf)
-        higher = pivot = jnp.max(scores, axis=1, keepdims=True)
+        higher = jnp.broadcast_to(jnp.max(scores, axis=1, keepdims=True), shape)
+        pivot = higher
     else:
-        here = jnp.where(alive, jnp.max(scores, axis=1, keepdims=True), -jnp.inf)
-        higher = jnp.maximum(carry[0], here)
+        here = jnp.broadcast_to(jnp.max(scores, axis=1, keepdims=True), shape)
+        higher = jnp.maximum(carry[0], jnp.where(alive, here, -jnp.inf))
         pivot = jnp.where(alive, higher, jnp.float32(1e30))
-    weights = jnp.exp2((scores - pivot) * factor)
-    total = jnp.sum(weights, axis=1, keepdims=True)
+    weights = jnp.exp2((scores - widen(pivot, width)) * factor)
+    total = jnp.broadcast_to(jnp.sum(weights, axis=1, keepdims=True), shape)
     mixed = jnp.dot(weights.astype(jnp.bfloat16), values, preferred_element_type=jnp.float32)
     if carry is None:
         return higher, total, mixed
@@ -38,8 +45,8 @@
     query = q_ref[...]
     rows = query.shape[0]
     if resumed:
-        carry = (refs[1][:, 0:1], refs[1][:, 1:2], refs[0][...])
-        refs = refs[2:]
+        carry = (refs[0][...], refs[1][...], refs[2][...])
+        refs = refs[3:]
     else:
         row = lax.broadcasted_iota(jnp.int32, (rows, rows), 0)
         column = lax.broadcasted_iota(jnp.int32, (rows, rows), 1)
@@ -53,9 +60,9 @@
     if last:
         refs[0][...] = (mixed / total).astype(jnp.bfloat16)
     else:
-        refs[0][...] = mixed
-        lane = lax.broadcasted_iota(jnp.int32, mixed.shape, 1)
-        refs[1][...] = jnp.where(lane == 0, peak, total)
+        refs[0][...] = peak
+        refs[1][...] = total
+        refs[2][...] = mixed
 
 
 def attend_stage(queries, sources, slots, live, state, last):
@@ -68,12 +75,12 @@
     shape = jax.ShapeDtypeStruct(queries.shape, jnp.float32)
     return pl.pallas_call(
         functools.partial(stage_kernel, state is None, state is not None, last, len(sources)),
-        out_shape=jax.ShapeDtypeStruct(queries.shape, jnp.bfloat16) if last else (shape, shape),
+        out_shape=jax.ShapeDtypeStruct(queries.shape, jnp.bfloat16) if last else (shape,) * 3,
         grid_spec=pltpu.PrefetchScalarGridSpec(
             num_scalar_prefetch=2,
             grid=(blocks, heads),
-            in_specs=[tile] + wholes + [tile] * (0 if state is None else 2),
-            out_specs=tile if last else (tile, tile),
+            in_specs=[tile] + wholes + [tile] * (0 if state is None else 3),
+            out_specs=tile if last else (tile,) * 3,
         ),
         compiler_params=pltpu.CompilerParams(vmem_limit_bytes=24 * 1024 * 1024),
         cost_estimate=pl.CostEstimate(

time: 193 us -> 172 us (0.89)
  Pallas kernels: 120 us -> 65 us
  waiting for transfers between devices: 20.3 us -> 50.3 us
  local copies, waits for them, and re-layouts: 15 us -> 18 us
    pallas_call x5, Pallas kernels: 110 us -> 54.5 us  [attend_stage(): pl.pallas_call(functools.partial(stage_kernel, state is None, state is no...]
    ppermute x17, waiting for transfers between devices: 20.3 us -> 50.3 us  [swap(): return lax.ppermute(array, axis, [(i, i ^ offset) for i in range(size)])]
    unnamed x15 -> x19, local copies, waits for them, and re-layouts: 7.24 us -> 10.2 us
  transfers between devices with their start and end apart: 20 -> 20, of which waited for: 6 -> 6; matrix products, arithmetic and copies ran while one was open for 6% -> 7% of each run, Pallas kernels for 57% -> 32%
where the time goes in v1:
time: 172 us; the launch traced here: 171 us
  Pallas kernels  65 us (38%)
  waiting for transfers between devices  50.3 us (29%)
  starting transfers between devices  24.8 us (14%)
  local copies, waits for them, and re-layouts  18 us (10%)
  between operations  7.87 us (5%)
  other arithmetic  5.06 us (3%)
    pallas_call x5, Pallas kernels, attend_stage(): pl.pallas_call(functools.partial(stage_kernel, state is None, state is no...  54.5 us
    ppermute x17, waiting for transfers between devices, swap(): return lax.ppermute(array, axis, [(i, i ^ offset) for i in range(size)])  50.3 us
    ppermute x17, starting transfers between devices, swap(): return lax.ppermute(array, axis, [(i, i ^ offset) for i in range(size)])  14.2 us
    ppermute x3, starting transfers between devices, whole_body(): chain.append(lax.ppermute(chain[-1], 'ctx', forward))  10.6 us
    pallas_call x1, Pallas kernels, project(): pl.pallas_call(functools.partial(project_kernel, plan, depth // 2), out_s...  10.5 us
    unnamed x19, local copies, waits for them, and re-layouts  10.2 us
    another operation x2, other arithmetic, whole_body(): jnp.stack([lookup_arrays.reshape(blocks_here, block_size, head_dim), cont...  3.5 us
  transfers between devices with their start and end apart: 20, of which 6 were waited for; matrix products, arithmetic and copies ran while one was open for 7% of the time, Pallas kernels for 32%

profile of v1, /device:TPU:0, one launch (start us, length us, event | category | flops | bytes accessed | tf_op | source)
XLA Modules:
  0.0 171.0 jit_solution(16176853302011591635)
XLA Ops:
  1.8 3.1 %collective-permute-start.3 = (s32[8]{0:T(128)S(1)}, s32[8]{0:T(128)S(1)}, u32[]{:S(2)}, u32[]{:S(2)}) collective-permute-start(s32[8]{0:T(128)S(1)} %fusion.1), channel_id=1, source_target_pairs={{0,4},{4,0},{8,12},{12,8},{16,20},{20,16},{24,28},{28,24},{1,5},{5... | collective-permute-start | bytes 104 | tf_op jit(solution)/shard_map/ppermute | solution.py:99
  4.9 1.9 %pad_maximum_fusion.refs_0_ = bf16[2,2,512,128]{3,2,1,0:T(8,128)(2,1)} fusion(bf16[1,2,512,128]{3,2,1,0:T(8,128)(2,1)} %bitcast.38, bf16[1,2,512,128]{3,2,1,0:T(8,128)(2,1)} %bitcast.40), kind=kLoop, calls=%fused_computation.2 | loop fusion | flops 262144 | bytes 1048576 | tf_op jit(solution)/shard_map/stack | solution.py:184
  6.8 4.3 %collective-permute-start = (bf16[2,2,512,128]{3,2,1,0:T(8,128)(2,1)}, bf16[2,2,512,128]{3,2,1,0:T(8,128)(2,1)}, u32[]{:S(2)}, u32[]{:S(2)}) collective-permute-start(bf16[2,2,512,128]{3,2,1,0:T(8,128)(2,1)} %pad_maximum_fusion.refs_0_), channel_id=1, source_target_pairs={{0,8},{4,12},{8,16},{12,20},{16,24},{20,28},{1,9},{5,13},{9,17},{1... | collective-permute-start | bytes 1572872 | tf_op jit(solution)/shard_map/ppermute | solution.py:211
  11.0 3.1 %constant_dynamic-slice_fusion = (bf16[128,4096]{1,0:T(8,128)(2,1)}, bf16[128,4096]{1,0:T(8,128)(2,1)}) fusion(bf16[512,4096]{1,0:T(8,128)(2,1)} %refs_4_.1, s32[]{:T(128)S(6)} %select_n.98, s32[]{:T(128)S(6)} %select_n.97), kind=kLoop, calls=%fused_computation.8 | loop fusion | bytes 4194312 | tf_op jit(solution)/shard_map/dynamic_slice | solution.py:110
  18.0 13.2 %shard_map.55 = (f32[1024,512]{1,0:T(8,128)S(1)}, f32[1024,512]{1,0:T(8,128)S(1)}, f32[1024,512]{1,0:T(8,128)S(1)}) custom-call(s32[2,2]{1,0:T(2,128)S(1)} %broadcast_in_dim.28.slots, s32[2,2]{1,0:T(2,128)S(1)} %and_convert_fusion.live, bf16[1024,512]{1,0:T(8,128)(2,1)S(1)} %bitcast.32, bf16[2,2,512,128]{3,2,1,0:T(8,128)(2,1)} %pad_maximum_fusion.refs_0_), custom_call_target="tpu_custom_call" | custom-call | flops 4294967296 | bytes 2097152 | tf_op jit(solution)/shard_map/pallas_call | solution.py:76
  35.7 3.6 %collective-permute-start.1 = (bf16[2,2,512,128]{3,2,1,0:T(8,128)(2,1)}, bf16[2,2,512,128]{3,2,1,0:T(8,128)(2,1)}, u32[]{:S(2)}, u32[]{:S(2)}) collective-permute-start(bf16[2,2,512,128]{3,2,1,0:T(8,128)(2,1)} %collective-permute-done.refs_0_), channel_id=1, source_target_pairs={{0,8},{4,12},{8,16},{12,20},{16,24},{20,28},{1,9},{5,13},{9,17},{1... | collective-permute-start | bytes 1572872 | tf_op jit(solution)/shard_map/ppermute | solution.py:211
  41.9 1.6 fusion
  51.6 1.6 collective-permute-start.6
  53.2 2.7 %collective-permute-start.2 = (bf16[2,2,512,128]{3,2,1,0:T(8,128)(2,1)}, bf16[2,2,512,128]{3,2,1,0:T(8,128)(2,1)S(1)}, u32[]{:S(2)}, u32[]{:S(2)}) collective-permute-start(bf16[2,2,512,128]{3,2,1,0:T(8,128)(2,1)} %collective-permute-done.1.refs_0_), channel_id=1, source_target_pairs={{0,8},{4,12},{8,16},{12,20},{16,24},{20,28},{1,9},{5,13},{9,17},{1... | collective-permute-start | bytes 1572872 | tf_op jit(solution)/shard_map/ppermute | solution.py:211
  55.9 1.6 copy-done.2
  57.5 1.6 copy-done.4
  59.1 1.6 copy-done.6
  60.7 11.9 %shard_map.56 = (f32[1024,512]{1,0:T(8,128)S(1)}, f32[1024,512]{1,0:T(8,128)S(1)}, f32[1024,512]{1,0:T(8,128)S(1)}) custom-call(s32[2,2]{1,0:T(2,128)S(1)} %stack.44.slots, s32[2,2]{1,0:T(2,128)S(1)} %add_convert_fusion.2.live, bf16[1024,512]{1,0:T(8,128)(2,1)S(1)} %bitcast.33, bf16[2,2,512,128]{3,2,1,0:T(8,128)(2,1)} %collective-permute-done.refs_0_, ...), custom_call_target="tpu_custom_call" | custom-call | flops 4294967296 | bytes 2097152 | tf_op jit(solution)/shard_map/pallas_call | solution.py:76
  74.1 1.5 collective-permute-start.13
  76.2 11.9 %shard_map.57 = (f32[1024,512]{1,0:T(8,128)S(1)}, f32[1024,512]{1,0:T(8,128)S(1)}, f32[1024,512]{1,0:T(8,128)S(1)}) custom-call(s32[2,2]{1,0:T(2,128)S(1)} %stack.41.slots, s32[2,2]{1,0:T(2,128)S(1)} %add_convert_fusion.1.live, bf16[1024,512]{1,0:T(8,128)(2,1)S(1)} %bitcast.34, bf16[2,2,512,128]{3,2,1,0:T(8,128)(2,1)} %collective-permute-done.1.refs_0_, ...), custom_call_target="tpu_custom_call" | custom-call | flops 4294967296 | bytes 2097152 | tf_op jit(solution)/shard_map/pallas_call | solution.py:76
  88.1 1.6 collective-permute-start.4
  89.7 11.0 %shard_map.58 = (f32[1024,512]{1,0:T(8,128)S(1)}, f32[1024,512]{1,0:T(8,128)S(1)}, f32[1024,512]{1,0:T(8,128)S(1)}) custom-call(s32[2,2]{1,0:T(2,128)S(1)} %stack.38.slots, s32[2,2]{1,0:T(2,128)S(1)} %add_convert_fusion.live, bf16[1024,512]{1,0:T(8,128)(2,1)S(1)} %bitcast.35, bf16[2,2,512,128]{3,2,1,0:T(8,128)(2,1)S(1)} %collective-permute-done.2.refs_0_, ...), custom_call_target="tpu_custom_call" | custom-call | flops 4294967296 | bytes 2097152 | tf_op jit(solution)/shard_map/pallas_call | solution.py:76
  100.6 30.5 %collective-permute-done.4.refs_0_ = bf16[2,1,512,128]{3,2,1,0:T(8,128)(2,1)S(1)} collective-permute-done((bf16[2,1,512,128]{3,2,1,0:T(8,128)(2,1)S(1)}, bf16[2,1,512,128]{3,2,1,0:T(8,128)(2,1)S(1)}, u32[]{:S(2)}, u32[]{:S(2)}) %collective-permute-start.4) | collective-permute-done | bytes 262176 | tf_op jit(solution)/shard_map/ppermute | solution.py:99
  131.2 6.6 %shard_map.59 = bf16[1024,512]{1,0:T(8,128)(2,1)S(1)} custom-call(s32[2,1]{1,0:T(2,128)S(1)} %broadcast_7_slots.2.slots, s32[2,1]{1,0:T(2,128)S(1)} %copy.27.live, bf16[1024,512]{1,0:T(8,128)(2,1)S(1)} %bitcast.36, bf16[2,1,512,128]{3,2,1,0:T(8,128)(2,1)S(1)} %collective-permute-done.4.refs_0_, f32[1024,512]{1,0:T(8,128)S(1)} %get-tuple-element.26.refs_1_, ...), custom_call_target="tpu_custom_call" | custom-call | flops 2147483648 | bytes 2097152 | tf_op jit(solution)/shard_map/pallas_call | solution.py:76
  138.0 1.6 collective-permute-start.8
  139.6 7.0 %collective-permute-done.10.refs_3_ = bf16[256,512]{1,0:T(8,128)(2,1)S(1)} collective-permute-done((bf16[256,512]{1,0:T(8,128)(2,1)S(1)}, bf16[256,512]{1,0:T(8,128)(2,1)S(1)}, u32[]{:S(2)}, u32[]{:S(2)}) %collective-permute-start.10) | collective-permute-done | bytes 262176 | tf_op jit(solution)/shard_map/ppermute | solution.py:99
  147.1 7.7 %collective-permute-done.9.refs_2_ = bf16[256,512]{1,0:T(8,128)(2,1)S(1)} collective-permute-done((bf16[256,512]{1,0:T(8,128)(2,1)S(1)}, bf16[256,512]{1,0:T(8,128)(2,1)S(1)}, u32[]{:S(2)}, u32[]{:S(2)}) %collective-permute-start.9) | collective-permute-done | bytes 262176 | tf_op jit(solution)/shard_map/ppermute | solution.py:99
  155.4 2.1 %collective-permute-done.18.refs_12_ = bf16[128,4096]{1,0:T(8,128)(2,1)S(1)} collective-permute-done((bf16[128,4096]{1,0:T(8,128)(2,1)S(1)}, bf16[128,4096]{1,0:T(8,128)(2,1)S(1)}, u32[]{:S(2)}, u32[]{:S(2)}) %collective-permute-start.18) | collective-permute-done | bytes 1048608 | tf_op jit(solution)/shard_map/ppermute | solution.py:99
  160.5 10.5 %project.1 = bf16[256,4096]{1,0:T(8,128)(2,1)} custom-call(s32[1]{0:T(128)} %bitcast.side_ref, bf16[256,512]{1,0:T(8,128)(2,1)S(1)} %get-tuple-element.42.refs_0_, bf16[256,512]{1,0:T(8,128)(2,1)S(1)} %collective-permute-done.8.refs_1_, bf16[256,512]{1,0:T(8,128)(2,1)S(1)} %collective-permute-done.9.refs_2_, ...), custom_call_target="tpu_custom_call" | custom-call | flops 4294967296 | bytes 16777216 | tf_op jit(solution)/shard_map/project/pallas_call | solution.py:157
  (83 shorter events, 19.5 us)
Async XLA Ops:
  1.8 37.6 %collective-permute-start.3 = (s32[8]{0:T(128)S(1)}, s32[8]{0:T(128)S(1)}, u32[]{:S(2)}, u32[]{:S(2)}) collective-permute-start(s32[8]{0:T(128)S(1)} %fusion.1), channel_id=1, source_target_pairs={{0,4},{4,0},{8,12},{12,8},{16,20},{20,16},{24,28},{28,24},{1,5},{5... | collective-permute-start | bytes 104 | tf_op jit(solution)/shard_map/ppermute | solution.py:99
  6.8 29.0 %collective-permute-start = (bf16[2,2,512,128]{3,2,1,0:T(8,128)(2,1)}, bf16[2,2,512,128]{3,2,1,0:T(8,128)(2,1)}, u32[]{:S(2)}, u32[]{:S(2)}) collective-permute-start(bf16[2,2,512,128]{3,2,1,0:T(8,128)(2,1)} %pad_maximum_fusion.refs_0_), channel_id=1, source_target_pairs={{0,8},{4,12},{8,16},{12,20},{16,24},{20,28},{1,9},{5,13},{9,17},{1... | collective-permute-start | bytes 1572872 | tf_op jit(solution)/shard_map/ppermute | solution.py:211
  11.0 149.5 %collective-permute-start.11 = (bf16[512,4096]{1,0:T(8,128)(2,1)}, bf16[512,4096]{1,0:T(8,128)(2,1)}, u32[]{:S(2)}, u32[]{:S(2)}) collective-permute-start(bf16[512,4096]{1,0:T(8,128)(2,1)} %refs_4_.1), channel_id=1, source_target_pairs={{0,1},{1,0},{2,3},{3,2},{4,5},{5,4},{6,7},{7,6},{8,9},{9,8},{10,11... | collective-permute-start | bytes 12582920 | tf_op jit(solution)/shard_map/ppermute | solution.py:99
  11.0 5.2 %copy-start.8 = (s32[2,1,6]{2,1,0:T(1,128)S(1)}, s32[2,1,6]{2,1,0:T(1,128)}, u32[]{:S(2)}) copy-start(s32[2,1,6]{2,1,0:T(1,128)} %param.8) | copy-start | bytes 148
  14.2 60.0 %collective-permute-start.12 = (bf16[128,4096]{1,0:T(8,128)(2,1)}, bf16[128,4096]{1,0:T(8,128)(2,1)S(1)}, u32[]{:S(2)}, u32[]{:S(2)}) collective-permute-start(bf16[128,4096]{1,0:T(8,128)(2,1)} %get-tuple-element.38), channel_id=1, source_target_pairs={{0,2},{1,3},{2,0},{3,1},{4,6},{5,7},{6,4},{7,5},{8,10},{9,11},{10,... | collective-permute-start | bytes 3145736 | tf_op jit(solution)/shard_map/ppermute | solution.py:99
  15.7 60.0 %collective-permute-start.14 = (bf16[128,4096]{1,0:T(8,128)(2,1)}, bf16[128,4096]{1,0:T(8,128)(2,1)S(1)}, u32[]{:S(2)}, u32[]{:S(2)}) collective-permute-start(bf16[128,4096]{1,0:T(8,128)(2,1)} %get-tuple-element.37), channel_id=1, source_target_pairs={{0,2},{1,3},{2,0},{3,1},{4,6},{5,7},{6,4},{7,5},{8,10},{9,11},{10,... | collective-permute-start | bytes 3145736 | tf_op jit(solution)/shard_map/ppermute | solution.py:99
  18.0 23.9 %copy-start.7 = (bf16[1024,1,128]{2,0,1:T(8,128)(2,1)S(1)}, bf16[1024,1,128]{2,0,1:T(8,128)(2,1)}, u32[]{:S(2)}) copy-start(bf16[1024,1,128]{2,0,1:T(8,128)(2,1)} %param.7) | copy-start | bytes 786436
  35.7 17.5 %collective-permute-start.1 = (bf16[2,2,512,128]{3,2,1,0:T(8,128)(2,1)}, bf16[2,2,512,128]{3,2,1,0:T(8,128)(2,1)}, u32[]{:S(2)}, u32[]{:S(2)}) collective-permute-start(bf16[2,2,512,128]{3,2,1,0:T(8,128)(2,1)} %collective-permute-done.refs_0_), channel_id=1, source_target_pairs={{0,8},{4,12},{8,16},{12,20},{16,24},{20,28},{1,9},{5,13},{9,17},{1... | collective-permute-start | bytes 1572872 | tf_op jit(solution)/shard_map/ppermute | solution.py:211
  43.6 8.1 %collective-permute-start.7 = (bf16[2,1,512,128]{3,2,1,0:T(8,128)(2,1)}, bf16[2,1,512,128]{3,2,1,0:T(8,128)(2,1)S(1)}, u32[]{:S(2)}, u32[]{:S(2)}) collective-permute-start(bf16[2,1,512,128]{3,2,1,0:T(8,128)(2,1)} %fusion), channel_id=1, source_target_pairs={{0,4},{4,0},{8,12},{12,8},{16,20},{20,16},{24,28},{28,24},{1,5},{5... | collective-permute-start | bytes 786440 | tf_op jit(solution)/shard_map/ppermute | solution.py:99
  51.6 21.9 %collective-permute-start.6 = (bf16[2,1,512,128]{3,2,1,0:T(8,128)(2,1)S(1)}, bf16[2,1,512,128]{3,2,1,0:T(8,128)(2,1)S(1)}, u32[]{:S(2)}, u32[]{:S(2)}) collective-permute-start(bf16[2,1,512,128]{3,2,1,0:T(8,128)(2,1)S(1)} %constant_dynamic-slice_fusion.6), channel_id=1, source_target_pairs={{0,4},{4,0},{8,12},{12,8},{16,20},{20,16},{24,28},{28,24},{1,5},{5... | collective-permute-start | bytes 786440 | tf_op jit(solution)/shard_map/ppermute | solution.py:99
  53.2 34.9 %collective-permute-start.2 = (bf16[2,2,512,128]{3,2,1,0:T(8,128)(2,1)}, bf16[2,2,512,128]{3,2,1,0:T(8,128)(2,1)S(1)}, u32[]{:S(2)}, u32[]{:S(2)}) collective-permute-start(bf16[2,2,512,128]{3,2,1,0:T(8,128)(2,1)} %collective-permute-done.1.refs_0_), channel_id=1, source_target_pairs={{0,8},{4,12},{8,16},{12,20},{16,24},{20,28},{1,9},{5,13},{9,17},{1... | collective-permute-start | bytes 1572872 | tf_op jit(solution)/shard_map/ppermute | solution.py:211
  55.9 1.6 copy-start.2
  73.6 16.1 %collective-permute-start.5 = (bf16[2,1,512,128]{3,2,1,0:T(8,128)(2,1)S(1)}, bf16[2,1,512,128]{3,2,1,0:T(8,128)(2,1)S(1)}, u32[]{:S(2)}, u32[]{:S(2)}) collective-permute-start(bf16[2,1,512,128]{3,2,1,0:T(8,128)(2,1)S(1)} %constant_dynamic-slice_fusion.7), channel_id=1, source_target_pairs={{0,4},{4,0},{8,12},{12,8},{16,20},{20,16},{24,28},{28,24},{1,5},{5... | collective-permute-start | bytes 786440 | tf_op jit(solution)/shard_map/ppermute | solution.py:99
  74.1 80.7 %collective-permute-start.13 = (bf16[128,4096]{1,0:T(8,128)(2,1)S(1)}, bf16[128,4096]{1,0:T(8,128)(2,1)S(1)}, u32[]{:S(2)}, u32[]{:S(2)}) collective-permute-start(bf16[128,4096]{1,0:T(8,128)(2,1)S(1)} %collective-permute-done.12.refs_6_), channel_id=1, source_target_pairs={{0,4},{4,0},{8,12},{12,8},{16,20},{20,16},{24,28},{28,24},{1,5},{5... | collective-permute-start | bytes 3145736 | tf_op jit(solution)/shard_map/ppermute | solution.py:99
  75.7 79.7 %collective-permute-start.15 = (bf16[128,4096]{1,0:T(8,128)(2,1)S(1)}, bf16[128,4096]{1,0:T(8,128)(2,1)S(1)}, u32[]{:S(2)}, u32[]{:S(2)}) collective-permute-start(bf16[128,4096]{1,0:T(8,128)(2,1)S(1)} %collective-permute-done.14.refs_8_), channel_id=1, source_target_pairs={{0,4},{4,0},{8,12},{12,8},{16,20},{20,16},{24,28},{28,24},{1,5},{5... | collective-permute-start | bytes 3145736 | tf_op jit(solution)/shard_map/ppermute | solution.py:99
  88.1 43.1 %collective-permute-start.4 = (bf16[2,1,512,128]{3,2,1,0:T(8,128)(2,1)S(1)}, bf16[2,1,512,128]{3,2,1,0:T(8,128)(2,1)S(1)}, u32[]{:S(2)}, u32[]{:S(2)}) collective-permute-start(bf16[2,1,512,128]{3,2,1,0:T(8,128)(2,1)S(1)} %constant_dynamic-slice_fusion.8), channel_id=1, source_target_pairs={{0,4},{4,0},{8,12},{12,8},{16,20},{20,16},{24,28},{28,24},{1,5},{5... | collective-permute-start | bytes 786440 | tf_op jit(solution)/shard_map/ppermute | solution.py:99
  131.2 29.3 %copy-start = (bf16[512,4096]{1,0:T(8,128)(2,1)S(1)}, bf16[512,4096]{1,0:T(8,128)(2,1)}, u32[]{:S(2)}) copy-start(bf16[512,4096]{1,0:T(8,128)(2,1)} %refs_4_.1) | copy-start | bytes 12582916
  137.9 8.6 %collective-permute-start.10 = (bf16[256,512]{1,0:T(8,128)(2,1)S(1)}, bf16[256,512]{1,0:T(8,128)(2,1)S(1)}, u32[]{:S(2)}, u32[]{:S(2)}) collective-permute-start(bf16[256,512]{1,0:T(8,128)(2,1)S(1)} %get-tuple-element.39), channel_id=1, source_target_pairs={{0,3},{1,2},{2,1},{3,0},{4,7},{5,6},{6,5},{7,4},{8,11},{9,10},{10,... | collective-permute-start | bytes 786440 | tf_op jit(solution)/shard_map/ppermute | solution.py:99
  138.0 9.2 %collective-permute-start.8 = (bf16[256,512]{1,0:T(8,128)(2,1)S(1)}, bf16[256,512]{1,0:T(8,128)(2,1)S(1)}, u32[]{:S(2)}, u32[]{:S(2)}) collective-permute-start(bf16[256,512]{1,0:T(8,128)(2,1)S(1)} %get-tuple-element.41), channel_id=1, source_target_pairs={{0,1},{1,0},{2,3},{3,2},{4,5},{5,4},{6,7},{7,6},{8,9},{9,8},{10,11... | collective-permute-start | bytes 786440 | tf_op jit(solution)/shard_map/ppermute | solution.py:99
  146.5 8.3 %collective-permute-start.9 = (bf16[256,512]{1,0:T(8,128)(2,1)S(1)}, bf16[256,512]{1,0:T(8,128)(2,1)S(1)}, u32[]{:S(2)}, u32[]{:S(2)}) collective-permute-start(bf16[256,512]{1,0:T(8,128)(2,1)S(1)} %get-tuple-element.40), channel_id=1, source_target_pairs={{0,2},{1,3},{2,0},{3,1},{4,6},{5,7},{6,4},{7,5},{8,10},{9,11},{10,... | collective-permute-start | bytes 786440 | tf_op jit(solution)/shard_map/ppermute | solution.py:99
  147.1 8.3 %collective-permute-start.16 = (bf16[128,4096]{1,0:T(8,128)(2,1)S(1)}, bf16[128,4096]{1,0:T(8,128)(2,1)S(1)}, u32[]{:S(2)}, u32[]{:S(2)}) collective-permute-start(bf16[128,4096]{1,0:T(8,128)(2,1)S(1)} %collective-permute-done.12.refs_6_), channel_id=1, source_target_pairs={{0,1},{1,0},{2,3},{3,2},{4,5},{5,4},{6,7},{7,6},{8,9},{9,8},{10,11... | collective-permute-start | bytes 3145736 | tf_op jit(solution)/shard_map/ppermute | solution.py:99
  154.8 2.7 %collective-permute-start.18 = (bf16[128,4096]{1,0:T(8,128)(2,1)S(1)}, bf16[128,4096]{1,0:T(8,128)(2,1)S(1)}, u32[]{:S(2)}, u32[]{:S(2)}) collective-permute-start(bf16[128,4096]{1,0:T(8,128)(2,1)S(1)} %collective-permute-done.14.refs_8_), channel_id=1, source_target_pairs={{0,1},{1,0},{2,3},{3,2},{4,5},{5,4},{6,7},{7,6},{8,9},{9,8},{10,11... | collective-permute-start | bytes 3145736 | tf_op jit(solution)/shard_map/ppermute | solution.py:99
  154.8 4.2 %collective-permute-start.17 = (bf16[128,4096]{1,0:T(8,128)(2,1)S(1)}, bf16[128,4096]{1,0:T(8,128)(2,1)S(1)}, u32[]{:S(2)}, u32[]{:S(2)}) collective-permute-start(bf16[128,4096]{1,0:T(8,128)(2,1)S(1)} %collective-permute-done.13.refs_7_), channel_id=1, source_target_pairs={{0,1},{1,0},{2,3},{3,2},{4,5},{5,4},{6,7},{7,6},{8,9},{9,8},{10,11... | collective-permute-start | bytes 3145736 | tf_op jit(solution)/shard_map/ppermute | solution.py:99
  155.4 5.1 %collective-permute-start.19 = (bf16[128,4096]{1,0:T(8,128)(2,1)S(1)}, bf16[128,4096]{1,0:T(8,128)(2,1)S(1)}, u32[]{:S(2)}, u32[]{:S(2)}) collective-permute-start(bf16[128,4096]{1,0:T(8,128)(2,1)S(1)} %collective-permute-done.15.refs_9_), channel_id=1, source_target_pairs={{0,1},{1,0},{2,3},{3,2},{4,5},{5,4},{6,7},{7,6},{8,9},{9,8},{10,11... | collective-permute-start | bytes 3145736 | tf_op jit(solution)/shard_map/ppermute | solution.py:99
  (5 other events, 7.2 us)

commit v2 on v1

--- a/solution.py
+++ b/solution.py
@@ -222,17 +222,21 @@
     live = named & (inside[None, :] < inside[:, None])
     state = attend_stage(flat_queries, [stacked], slots, live.astype(jnp.int32), None, False)
     twin = position ^ 1
+    sources, places, lives = [], [], []
     for turn in range(1, rounds + 2):
         direct, direct_live = wanted_from(position - 2 * turn)
         _, side_live = wanted_from(twin - 2 * (turn - 1))
         none = jnp.zeros_like(direct)
         last = turn == rounds + 1
-        sources = [sides[turn - 1]] if last else [chain[turn], sides[turn - 1]]
-        places = [none] if last else [direct, none]
-        lives = [side_live] if last else [direct_live, side_live]
+        sources += [sides[turn - 1]] if last else [chain[turn], sides[turn - 1]]
+        places += [none] if last else [direct, none]
+        lives += [side_live] if last else [direct_live, side_live]
+        if turn % 2 and not last:
+            continue
         state = attend_stage(
             flat_queries, sources, jnp.stack(places, axis=1), jnp.stack(lives, axis=1), state, last
         )
+        sources, places, lives = [], [], []
     flat_rows = state
     head_count = lax.axis_size("head")
     head = lax.axis_index("head")

time: 172 us -> 178 us (1.035)
  waiting for transfers between devices: 50.3 us -> 61.2 us
  Pallas kernels: 65 us -> 58 us
    ppermute x3, waiting for transfers between devices: 0.01 us -> 11.4 us  [whole_body(): chain.append(lax.ppermute(chain[-1], 'ctx', forward))]
    pallas_call x5 -> x3, Pallas kernels: 54.5 us -> 47.5 us  [attend_stage(): pl.pallas_call(functools.partial(stage_kernel, state is None, state is no...]
    ppermute x3, starting transfers between devices: 10.6 us -> 13 us  [whole_body(): chain.append(lax.ppermute(chain[-1], 'ctx', forward))]
  transfers between devices with their start and end apart: 20 -> 20, of which waited for: 6 -> 8; matrix products, arithmetic and copies ran while one was open for 7% -> 8% of each run, Pallas kernels for 32% -> 27%
where the time goes in v2:
time: 178 us; the launch traced here: 177 us
  waiting for transfers between devices  61.2 us (34%)
  Pallas kernels  58 us (33%)
  starting transfers between devices  26.1 us (15%)
  local copies, waits for them, and re-layouts  19.6 us (11%)
  between operations  7.51 us (4%)
  other arithmetic  5.07 us (3%)
    ppermute x17, waiting for transfers between devices, swap(): return lax.ppermute(array, axis, [(i, i ^ offset) for i in range(size)])  49.8 us
    pallas_call x3, Pallas kernels, attend_stage(): pl.pallas_call(functools.partial(stage_kernel, state is None, state is no...  47.5 us
    ppermute x17, starting transfers between devices, swap(): return lax.ppermute(array, axis, [(i, i ^ offset) for i in range(size)])  13.1 us
    ppermute x3, starting transfers between devices, whole_body(): chain.append(lax.ppermute(chain[-1], 'ctx', forward))  13 us
    ppermute x3, waiting for transfers between devices, whole_body(): chain.append(lax.ppermute(chain[-1], 'ctx', forward))  11.4 us
    pallas_call x1, Pallas kernels, project(): pl.pallas_call(functools.partial(project_kernel, plan, depth // 2), out_s...  10.5 us
    unnamed x19, local copies, waits for them, and re-layouts  10.2 us
    dynamic_slice x3, local copies, waits for them, and re-layouts, whole_body(): picked = lax.dynamic_slice_in_dim(chain[-1], place, 1, 1)  3.63 us
  transfers between devices with their start and end apart: 20, of which 8 were waited for; matrix products, arithmetic and copies ran while one was open for 8% of the time, Pallas kernels for 27%

profile of v2, /device:TPU:0, one launch (start us, length us, event | category | flops | bytes accessed | tf_op | source)
XLA Modules:
  0.0 177.5 jit_solution(5717285780483633842)
XLA Ops:
  1.8 3.1 %collective-permute-start.3 = (s32[8]{0:T(128)S(1)}, s32[8]{0:T(128)S(1)}, u32[]{:S(2)}, u32[]{:S(2)}) collective-permute-start(s32[8]{0:T(128)S(1)} %fusion.1), channel_id=1, source_target_pairs={{0,4},{4,0},{8,12},{12,8},{16,20},{20,16},{24,28},{28,24},{1,5},{5... | collective-permute-start | bytes 104 | tf_op jit(solution)/shard_map/ppermute | solution.py:99
  4.9 1.9 %pad_maximum_fusion.refs_0_ = bf16[2,2,512,128]{3,2,1,0:T(8,128)(2,1)} fusion(bf16[1,2,512,128]{3,2,1,0:T(8,128)(2,1)} %bitcast.36, bf16[1,2,512,128]{3,2,1,0:T(8,128)(2,1)} %bitcast.38), kind=kLoop, calls=%fused_computation.2 | loop fusion | flops 262144 | bytes 1048576 | tf_op jit(solution)/shard_map/stack | solution.py:184
  6.7 4.3 %collective-permute-start = (bf16[2,2,512,128]{3,2,1,0:T(8,128)(2,1)}, bf16[2,2,512,128]{3,2,1,0:T(8,128)(2,1)}, u32[]{:S(2)}, u32[]{:S(2)}) collective-permute-start(bf16[2,2,512,128]{3,2,1,0:T(8,128)(2,1)} %pad_maximum_fusion.refs_0_), channel_id=1, source_target_pairs={{0,8},{4,12},{8,16},{12,20},{16,24},{20,28},{1,9},{5,13},{9,17},{1... | collective-permute-start | bytes 1572872 | tf_op jit(solution)/shard_map/ppermute | solution.py:211
  11.0 3.1 %constant_dynamic-slice_fusion = (bf16[128,4096]{1,0:T(8,128)(2,1)}, bf16[128,4096]{1,0:T(8,128)(2,1)}) fusion(bf16[512,4096]{1,0:T(8,128)(2,1)} %refs_4_.1, s32[]{:T(128)S(6)} %select_n.98, s32[]{:T(128)S(6)} %select_n.97), kind=kLoop, calls=%fused_computation.8 | loop fusion | bytes 4194312 | tf_op jit(solution)/shard_map/dynamic_slice | solution.py:110
  18.1 13.2 %shard_map.55 = (f32[1024,512]{1,0:T(8,128)S(1)}, f32[1024,512]{1,0:T(8,128)S(1)}, f32[1024,512]{1,0:T(8,128)S(1)}) custom-call(s32[2,2]{1,0:T(2,128)S(1)} %broadcast_in_dim.28.slots, s32[2,2]{1,0:T(2,128)S(1)} %and_convert_fusion.live, bf16[1024,512]{1,0:T(8,128)(2,1)S(1)} %bitcast.32, bf16[2,2,512,128]{3,2,1,0:T(8,128)(2,1)} %pad_maximum_fusion.refs_0_), custom_call_target="tpu_custom_call" | custom-call | flops 4294967296 | bytes 2097152 | tf_op jit(solution)/shard_map/pallas_call | solution.py:76
  35.3 3.6 %collective-permute-start.1 = (bf16[2,2,512,128]{3,2,1,0:T(8,128)(2,1)}, bf16[2,2,512,128]{3,2,1,0:T(8,128)(2,1)}, u32[]{:S(2)}, u32[]{:S(2)}) collective-permute-start(bf16[2,2,512,128]{3,2,1,0:T(8,128)(2,1)} %collective-permute-done.refs_0_), channel_id=1, source_target_pairs={{0,8},{4,12},{8,16},{12,20},{16,24},{20,28},{1,9},{5,13},{9,17},{1... | collective-permute-start | bytes 1572872 | tf_op jit(solution)/shard_map/ppermute | solution.py:211
  39.9 9.7 %collective-permute-done.1.refs_2_ = bf16[2,2,512,128]{3,2,1,0:T(8,128)(2,1)} collective-permute-done((bf16[2,2,512,128]{3,2,1,0:T(8,128)(2,1)}, bf16[2,2,512,128]{3,2,1,0:T(8,128)(2,1)}, u32[]{:S(2)}, u32[]{:S(2)}) %collective-permute-start.1) | collective-permute-done | bytes 524320 | tf_op jit(solution)/shard_map/ppermute | solution.py:211
  49.6 5.2 %collective-permute-start.2 = (bf16[2,2,512,128]{3,2,1,0:T(8,128)(2,1)}, bf16[2,2,512,128]{3,2,1,0:T(8,128)(2,1)}, u32[]{:S(2)}, u32[]{:S(2)}) collective-permute-start(bf16[2,2,512,128]{3,2,1,0:T(8,128)(2,1)} %collective-permute-done.1.refs_2_), channel_id=1, source_target_pairs={{0,8},{4,12},{8,16},{12,20},{16,24},{20,28},{1,9},{5,13},{9,17},{1... | collective-permute-start | bytes 1572872 | tf_op jit(solution)/shard_map/ppermute | solution.py:211
  58.5 1.6 fusion
  61.3 1.7 constant_dynamic-slice_fusion.6
  62.9 1.7 collective-permute-done.2.refs_0_
  71.0 1.6 collective-permute-start.4
  73.1 1.5 collective-permute-start.15
  75.2 1.6 copy-done.2
  76.8 1.6 copy-done.4
  78.4 1.6 copy-done.6
  79.9 19.2 %shard_map.56 = (f32[1024,512]{1,0:T(8,128)S(1)}, f32[1024,512]{1,0:T(8,128)S(1)}, f32[1024,512]{1,0:T(8,128)S(1)}) custom-call(s32[2,4]{1,0:T(2,128)S(1)} %pad_add_fusion.slots, s32[2,4]{1,0:T(2,128)S(1)} %add_convert_fusion.1.live, bf16[1024,512]{1,0:T(8,128)(2,1)S(1)} %bitcast.33, bf16[2,2,512,128]{3,2,1,0:T(8,128)(2,1)} %collective-permute-done.refs_0_, ...), custom_call_target="tpu_custom_call" | custom-call | flops 8589934592 | bytes 2097152 | tf_op jit(solution)/shard_map/pallas_call | solution.py:76
  99.2 30.0 %collective-permute-done.5.refs_2_ = bf16[2,1,512,128]{3,2,1,0:T(8,128)(2,1)S(1)} collective-permute-done((bf16[2,1,512,128]{3,2,1,0:T(8,128)(2,1)S(1)}, bf16[2,1,512,128]{3,2,1,0:T(8,128)(2,1)S(1)}, u32[]{:S(2)}, u32[]{:S(2)}) %collective-permute-start.5) | collective-permute-done | bytes 262176 | tf_op jit(solution)/shard_map/ppermute | solution.py:99
  129.2 15.1 %shard_map.57 = bf16[1024,512]{1,0:T(8,128)(2,1)S(1)} custom-call(s32[2,3]{1,0:T(2,128)S(1)} %stack.14.slots, s32[2,3]{1,0:T(2,128)S(1)} %add_convert_fusion.live, bf16[1024,512]{1,0:T(8,128)(2,1)S(1)} %bitcast.34, bf16[2,2,512,128]{3,2,1,0:T(8,128)(2,1)} %collective-permute-done.2.refs_0_, bf16[2,1,512,128]{3,2,1,0:T(8,128)(2,1)S(1)} %collective-permute-done.4.refs_1_, ...), custom_call_target="tpu_custom_call" | custom-call | flops 6442450944 | bytes 2097152 | tf_op jit(solution)/shard_map/pallas_call | solution.py:76
  144.4 1.6 collective-permute-start.8
  146.0 7.0 %collective-permute-done.10.refs_3_ = bf16[256,512]{1,0:T(8,128)(2,1)S(1)} collective-permute-done((bf16[256,512]{1,0:T(8,128)(2,1)S(1)}, bf16[256,512]{1,0:T(8,128)(2,1)S(1)}, u32[]{:S(2)}, u32[]{:S(2)}) %collective-permute-start.10) | collective-permute-done | bytes 262176 | tf_op jit(solution)/shard_map/ppermute | solution.py:99
  153.6 7.7 %collective-permute-done.9.refs_2_ = bf16[256,512]{1,0:T(8,128)(2,1)S(1)} collective-permute-done((bf16[256,512]{1,0:T(8,128)(2,1)S(1)}, bf16[256,512]{1,0:T(8,128)(2,1)S(1)}, u32[]{:S(2)}, u32[]{:S(2)}) %collective-permute-start.9) | collective-permute-done | bytes 262176 | tf_op jit(solution)/shard_map/ppermute | solution.py:99
  161.9 2.1 %collective-permute-done.18.refs_12_ = bf16[128,4096]{1,0:T(8,128)(2,1)S(1)} collective-permute-done((bf16[128,4096]{1,0:T(8,128)(2,1)S(1)}, bf16[128,4096]{1,0:T(8,128)(2,1)S(1)}, u32[]{:S(2)}, u32[]{:S(2)}) %collective-permute-start.18) | collective-permute-done | bytes 1048608 | tf_op jit(solution)/shard_map/ppermute | solution.py:99
  167.0 10.5 %project.1 = bf16[256,4096]{1,0:T(8,128)(2,1)} custom-call(s32[1]{0:T(128)} %bitcast.side_ref, bf16[256,512]{1,0:T(8,128)(2,1)S(1)} %get-tuple-element.30.refs_0_, bf16[256,512]{1,0:T(8,128)(2,1)S(1)} %collective-permute-done.8.refs_1_, bf16[256,512]{1,0:T(8,128)(2,1)S(1)} %collective-permute-done.9.refs_2_, ...), custom_call_target="tpu_custom_call" | custom-call | flops 4294967296 | bytes 16777216 | tf_op jit(solution)/shard_map/project/pallas_call | solution.py:157
  (79 shorter events, 19.9 us)
Async XLA Ops:
  1.8 53.0 %collective-permute-start.3 = (s32[8]{0:T(128)S(1)}, s32[8]{0:T(128)S(1)}, u32[]{:S(2)}, u32[]{:S(2)}) collective-permute-start(s32[8]{0:T(128)S(1)} %fusion.1), channel_id=1, source_target_pairs={{0,4},{4,0},{8,12},{12,8},{16,20},{20,16},{24,28},{28,24},{1,5},{5... | collective-permute-start | bytes 104 | tf_op jit(solution)/shard_map/ppermute | solution.py:99
  6.7 28.5 %collective-permute-start = (bf16[2,2,512,128]{3,2,1,0:T(8,128)(2,1)}, bf16[2,2,512,128]{3,2,1,0:T(8,128)(2,1)}, u32[]{:S(2)}, u32[]{:S(2)}) collective-permute-start(bf16[2,2,512,128]{3,2,1,0:T(8,128)(2,1)} %pad_maximum_fusion.refs_0_), channel_id=1, source_target_pairs={{0,8},{4,12},{8,16},{12,20},{16,24},{20,28},{1,9},{5,13},{9,17},{1... | collective-permute-start | bytes 1572872 | tf_op jit(solution)/shard_map/ppermute | solution.py:211
  11.0 156.0 %collective-permute-start.11 = (bf16[512,4096]{1,0:T(8,128)(2,1)}, bf16[512,4096]{1,0:T(8,128)(2,1)}, u32[]{:S(2)}, u32[]{:S(2)}) collective-permute-start(bf16[512,4096]{1,0:T(8,128)(2,1)} %refs_4_.1), channel_id=1, source_target_pairs={{0,1},{1,0},{2,3},{3,2},{4,5},{5,4},{6,7},{7,6},{8,9},{9,8},{10,11... | collective-permute-start | bytes 12582920 | tf_op jit(solution)/shard_map/ppermute | solution.py:99
  11.0 5.2 %copy-start.8 = (s32[2,1,6]{2,1,0:T(1,128)S(1)}, s32[2,1,6]{2,1,0:T(1,128)}, u32[]{:S(2)}) copy-start(s32[2,1,6]{2,1,0:T(1,128)} %param.8) | copy-start | bytes 148
  14.2 58.5 %collective-permute-start.12 = (bf16[128,4096]{1,0:T(8,128)(2,1)}, bf16[128,4096]{1,0:T(8,128)(2,1)S(1)}, u32[]{:S(2)}, u32[]{:S(2)}) collective-permute-start(bf16[128,4096]{1,0:T(8,128)(2,1)} %get-tuple-element.26), channel_id=1, source_target_pairs={{0,2},{1,3},{2,0},{3,1},{4,6},{5,7},{6,4},{7,5},{8,10},{9,11},{10,... | collective-permute-start | bytes 3145736 | tf_op jit(solution)/shard_map/ppermute | solution.py:99
  15.7 57.5 %collective-permute-start.14 = (bf16[128,4096]{1,0:T(8,128)(2,1)}, bf16[128,4096]{1,0:T(8,128)(2,1)S(1)}, u32[]{:S(2)}, u32[]{:S(2)}) collective-permute-start(bf16[128,4096]{1,0:T(8,128)(2,1)} %get-tuple-element.25), channel_id=1, source_target_pairs={{0,2},{1,3},{2,0},{3,1},{4,6},{5,7},{6,4},{7,5},{8,10},{9,11},{10,... | collective-permute-start | bytes 3145736 | tf_op jit(solution)/shard_map/ppermute | solution.py:99
  18.0 40.5 %copy-start.7 = (bf16[1024,1,128]{2,0,1:T(8,128)(2,1)S(1)}, bf16[1024,1,128]{2,0,1:T(8,128)(2,1)}, u32[]{:S(2)}) copy-start(bf16[1024,1,128]{2,0,1:T(8,128)(2,1)} %param.7) | copy-start | bytes 786436
  35.3 14.3 %collective-permute-start.1 = (bf16[2,2,512,128]{3,2,1,0:T(8,128)(2,1)}, bf16[2,2,512,128]{3,2,1,0:T(8,128)(2,1)}, u32[]{:S(2)}, u32[]{:S(2)}) collective-permute-start(bf16[2,2,512,128]{3,2,1,0:T(8,128)(2,1)} %collective-permute-done.refs_0_), channel_id=1, source_target_pairs={{0,8},{4,12},{8,16},{12,20},{16,24},{20,28},{1,9},{5,13},{9,17},{1... | collective-permute-start | bytes 1572872 | tf_op jit(solution)/shard_map/ppermute | solution.py:211
  49.6 15.1 %collective-permute-start.2 = (bf16[2,2,512,128]{3,2,1,0:T(8,128)(2,1)}, bf16[2,2,512,128]{3,2,1,0:T(8,128)(2,1)}, u32[]{:S(2)}, u32[]{:S(2)}) collective-permute-start(bf16[2,2,512,128]{3,2,1,0:T(8,128)(2,1)} %collective-permute-done.1.refs_2_), channel_id=1, source_target_pairs={{0,8},{4,12},{8,16},{12,20},{16,24},{20,28},{1,9},{5,13},{9,17},{1... | collective-permute-start | bytes 1572872 | tf_op jit(solution)/shard_map/ppermute | solution.py:211
  60.2 10.8 %collective-permute-start.6 = (bf16[2,1,512,128]{3,2,1,0:T(8,128)(2,1)}, bf16[2,1,512,128]{3,2,1,0:T(8,128)(2,1)S(1)}, u32[]{:S(2)}, u32[]{:S(2)}) collective-permute-start(bf16[2,1,512,128]{3,2,1,0:T(8,128)(2,1)} %fusion), channel_id=1, source_target_pairs={{0,4},{4,0},{8,12},{12,8},{16,20},{20,16},{24,28},{28,24},{1,5},{5... | collective-permute-start | bytes 786440 | tf_op jit(solution)/shard_map/ppermute | solution.py:99
  64.7 10.0 %collective-permute-start.7 = (bf16[2,1,512,128]{3,2,1,0:T(8,128)(2,1)}, bf16[2,1,512,128]{3,2,1,0:T(8,128)(2,1)}, u32[]{:S(2)}, u32[]{:S(2)}) collective-permute-start(bf16[2,1,512,128]{3,2,1,0:T(8,128)(2,1)} %constant_dynamic-slice_fusion.6), channel_id=1, source_target_pairs={{0,4},{4,0},{8,12},{12,8},{16,20},{20,16},{24,28},{28,24},{1,5},{5... | collective-permute-start | bytes 786440 | tf_op jit(solution)/shard_map/ppermute | solution.py:99
  71.0 28.1 %collective-permute-start.4 = (bf16[2,1,512,128]{3,2,1,0:T(8,128)(2,1)S(1)}, bf16[2,1,512,128]{3,2,1,0:T(8,128)(2,1)S(1)}, u32[]{:S(2)}, u32[]{:S(2)}) collective-permute-start(bf16[2,1,512,128]{3,2,1,0:T(8,128)(2,1)S(1)} %constant_dynamic-slice_fusion.8), channel_id=1, source_target_pairs={{0,4},{4,0},{8,12},{12,8},{16,20},{20,16},{24,28},{28,24},{1,5},{5... | collective-permute-start | bytes 786440 | tf_op jit(solution)/shard_map/ppermute | solution.py:99
  72.6 88.7 %collective-permute-start.13 = (bf16[128,4096]{1,0:T(8,128)(2,1)S(1)}, bf16[128,4096]{1,0:T(8,128)(2,1)S(1)}, u32[]{:S(2)}, u32[]{:S(2)}) collective-permute-start(bf16[128,4096]{1,0:T(8,128)(2,1)S(1)} %collective-permute-done.12.refs_6_), channel_id=1, source_target_pairs={{0,4},{4,0},{8,12},{12,8},{16,20},{20,16},{24,28},{28,24},{1,5},{5... | collective-permute-start | bytes 3145736 | tf_op jit(solution)/shard_map/ppermute | solution.py:99
  73.1 88.7 %collective-permute-start.15 = (bf16[128,4096]{1,0:T(8,128)(2,1)S(1)}, bf16[128,4096]{1,0:T(8,128)(2,1)S(1)}, u32[]{:S(2)}, u32[]{:S(2)}) collective-permute-start(bf16[128,4096]{1,0:T(8,128)(2,1)S(1)} %collective-permute-done.14.refs_8_), channel_id=1, source_target_pairs={{0,4},{4,0},{8,12},{12,8},{16,20},{20,16},{24,28},{28,24},{1,5},{5... | collective-permute-start | bytes 3145736 | tf_op jit(solution)/shard_map/ppermute | solution.py:99
  74.7 54.5 %collective-permute-start.5 = (bf16[2,1,512,128]{3,2,1,0:T(8,128)(2,1)S(1)}, bf16[2,1,512,128]{3,2,1,0:T(8,128)(2,1)S(1)}, u32[]{:S(2)}, u32[]{:S(2)}) collective-permute-start(bf16[2,1,512,128]{3,2,1,0:T(8,128)(2,1)S(1)} %constant_dynamic-slice_fusion.7), channel_id=1, source_target_pairs={{0,4},{4,0},{8,12},{12,8},{16,20},{20,16},{24,28},{28,24},{1,5},{5... | collective-permute-start | bytes 786440 | tf_op jit(solution)/shard_map/ppermute | solution.py:99
  75.2 1.6 copy-start.2
  129.2 37.8 %copy-start = (bf16[512,4096]{1,0:T(8,128)(2,1)S(1)}, bf16[512,4096]{1,0:T(8,128)(2,1)}, u32[]{:S(2)}) copy-start(bf16[512,4096]{1,0:T(8,128)(2,1)} %refs_4_.1) | copy-start | bytes 12582916
  144.3 8.6 %collective-permute-start.10 = (bf16[256,512]{1,0:T(8,128)(2,1)S(1)}, bf16[256,512]{1,0:T(8,128)(2,1)S(1)}, u32[]{:S(2)}, u32[]{:S(2)}) collective-permute-start(bf16[256,512]{1,0:T(8,128)(2,1)S(1)} %get-tuple-element.27), channel_id=1, source_target_pairs={{0,3},{1,2},{2,1},{3,0},{4,7},{5,6},{6,5},{7,4},{8,11},{9,10},{10,... | collective-permute-start | bytes 786440 | tf_op jit(solution)/shard_map/ppermute | solution.py:99
  144.4 9.2 %collective-permute-start.8 = (bf16[256,512]{1,0:T(8,128)(2,1)S(1)}, bf16[256,512]{1,0:T(8,128)(2,1)S(1)}, u32[]{:S(2)}, u32[]{:S(2)}) collective-permute-start(bf16[256,512]{1,0:T(8,128)(2,1)S(1)} %get-tuple-element.29), channel_id=1, source_target_pairs={{0,1},{1,0},{2,3},{3,2},{4,5},{5,4},{6,7},{7,6},{8,9},{9,8},{10,11... | collective-permute-start | bytes 786440 | tf_op jit(solution)/shard_map/ppermute | solution.py:99
  153.0 8.3 %collective-permute-start.9 = (bf16[256,512]{1,0:T(8,128)(2,1)S(1)}, bf16[256,512]{1,0:T(8,128)(2,1)S(1)}, u32[]{:S(2)}, u32[]{:S(2)}) collective-permute-start(bf16[256,512]{1,0:T(8,128)(2,1)S(1)} %get-tuple-element.28), channel_id=1, source_target_pairs={{0,2},{1,3},{2,0},{3,1},{4,6},{5,7},{6,4},{7,5},{8,10},{9,11},{10,... | collective-permute-start | bytes 786440 | tf_op jit(solution)/shard_map/ppermute | solution.py:99
  153.6 8.3 %collective-permute-start.16 = (bf16[128,4096]{1,0:T(8,128)(2,1)S(1)}, bf16[128,4096]{1,0:T(8,128)(2,1)S(1)}, u32[]{:S(2)}, u32[]{:S(2)}) collective-permute-start(bf16[128,4096]{1,0:T(8,128)(2,1)S(1)} %collective-permute-done.12.refs_6_), channel_id=1, source_target_pairs={{0,1},{1,0},{2,3},{3,2},{4,5},{5,4},{6,7},{7,6},{8,9},{9,8},{10,11... | collective-permute-start | bytes 3145736 | tf_op jit(solution)/shard_map/ppermute | solution.py:99
  161.3 2.7 %collective-permute-start.18 = (bf16[128,4096]{1,0:T(8,128)(2,1)S(1)}, bf16[128,4096]{1,0:T(8,128)(2,1)S(1)}, u32[]{:S(2)}, u32[]{:S(2)}) collective-permute-start(bf16[128,4096]{1,0:T(8,128)(2,1)S(1)} %collective-permute-done.14.refs_8_), channel_id=1, source_target_pairs={{0,1},{1,0},{2,3},{3,2},{4,5},{5,4},{6,7},{7,6},{8,9},{9,8},{10,11... | collective-permute-start | bytes 3145736 | tf_op jit(solution)/shard_map/ppermute | solution.py:99
  161.3 4.2 %collective-permute-start.17 = (bf16[128,4096]{1,0:T(8,128)(2,1)S(1)}, bf16[128,4096]{1,0:T(8,128)(2,1)S(1)}, u32[]{:S(2)}, u32[]{:S(2)}) collective-permute-start(bf16[128,4096]{1,0:T(8,128)(2,1)S(1)} %collective-permute-done.13.refs_7_), channel_id=1, source_target_pairs={{0,1},{1,0},{2,3},{3,2},{4,5},{5,4},{6,7},{7,6},{8,9},{9,8},{10,11... | collective-permute-start | bytes 3145736 | tf_op jit(solution)/shard_map/ppermute | solution.py:99
  161.8 5.1 %collective-permute-start.19 = (bf16[128,4096]{1,0:T(8,128)(2,1)S(1)}, bf16[128,4096]{1,0:T(8,128)(2,1)S(1)}, u32[]{:S(2)}, u32[]{:S(2)}) collective-permute-start(bf16[128,4096]{1,0:T(8,128)(2,1)S(1)} %collective-permute-done.15.refs_9_), channel_id=1, source_target_pairs={{0,1},{1,0},{2,3},{3,2},{4,5},{5,4},{6,7},{7,6},{8,9},{9,8},{10,11... | collective-permute-start | bytes 3145736 | tf_op jit(solution)/shard_map/ppermute | solution.py:99
  (5 other events, 7.2 us)
